TPU v7x, 32 devices: a whole 2x2x4 slice. The times are simulated.
32 devices in a mesh: tm: 16 (over z, y, x), state: 2 (over core).
Axes of the slice: x: 2, y: 2, z: 4, core: 2. Of those that a mesh axis runs over, the one named last changes fastest.
Arguments:
- symbols: int32 [8], P('state'), may hold values from 0 to 255
- emission: float32 [8192, 256], P('tm'), may hold values from 0.2 to 5
- decay: float32 [2, 8192], P('state', 'tm'), may hold values from 0.05 to 1
- left_factor: float32 [2, 64, 8192], P('state', None, 'tm'), may hold values from 0.1 to 3
- right_factor: float32 [2, 64, 8192], P('state', None, 'tm'), may hold values from 0.001 to 0.03
- initial: float32 [8192], P('tm'), may hold values from 0.1 to 10
Outputs:
- filtered: float32 [8, 8192], P('state', 'tm')
- log_scale: float32 [8], P('state')
All inputs are finite; a program needn't handle non-finite values.
Results may differ from a plain program's by a relative error of at most 0.00011.
Values sent between devices are 32-bit elements; how exact they have to be, the bound alone decides.
A program may use at most 64 MiB of HBM per device.

v0:
```python
import jax
import jax.numpy as jnp
from jax import lax
from jax.sharding import PartitionSpec as P

S = 8192


PRECISE = lax.Precision.HIGHEST


def passed_along(value, axis, steps):
    count = lax.axis_size(axis)
    first, last = (max(0, -steps), min(count, count - steps))
    return lax.ppermute(value, axis, [(source, source + steps) for source in range(first, last)])


def run_span(entry_vec, emitted_all, decay_row, left_rows, right_rows):
    projected, total_sum = lax.psum(
        (jnp.dot(left_rows, entry_vec, precision=PRECISE), jnp.sum(entry_vec)), "tm"
    )
    rescale = S / total_sum
    belief = entry_vec * rescale
    mixture = projected * rescale / S

    def frame(state_pair, emitted):
        belief_now, mixture_now = state_pair
        unscaled = emitted * (
            decay_row * belief_now + jnp.dot(mixture_now, right_rows, precision=PRECISE)
        )
        proj_next, total_next = lax.psum(
            (jnp.dot(left_rows, unscaled, precision=PRECISE), jnp.sum(unscaled)), "tm"
        )
        normal = total_next / S
        belief_next = unscaled / normal
        mixture_next = proj_next / normal / S
        return ((belief_next, mixture_next), (belief_next, jnp.log(normal)))

    (closing, mixture_end), (beliefs, log_levels) = lax.scan(frame, (belief, mixture), emitted_all)
    return (beliefs, log_levels, closing)


def span_map(emitted_all, decay_row, left_rows, right_rows):
    frames = emitted_all.shape[0]
    rank_cols = left_rows.shape[0]
    cells = left_rows.shape[1]
    growth = emitted_all * decay_row[None, :]
    markers = jnp.eye(frames, dtype=jnp.float32)

    def advance(state_pair, inputs):
        reached, weights = state_pair
        grow_row, emitted, marker = inputs
        weights_next = weights * grow_row[None, :] + marker[:, None] * emitted[None, :]
        return ((reached * grow_row, weights_next), (reached, weights_next))

    begin_pair = (jnp.ones((cells,), jnp.float32), jnp.zeros((frames, cells), jnp.float32))
    (final_reach, final_weights), (reached_all, weights_all) = lax.scan(
        advance, begin_pair, (growth, emitted_all, markers)
    )
    probes = (left_rows[None, :, :] * reached_all[:, None, :]).reshape(
        frames * rank_cols, cells
    ) / S
    vb_rows = right_rows[None, :, :] * final_weights[:, None, :]
    pair_rows = weights_all[: frames - 1].reshape((frames - 1) * frames, cells)
    group_size = max(rank_cols // 8, 1)
    blocks = []
    for offset in range(0, rank_cols, group_size):
        cross_rows = (
            left_rows[offset : offset + group_size, None, :] * right_rows[None, :, :]
        ).reshape(-1, cells)
        blocks.append(jnp.einsum("pw,qw->pq", pair_rows, cross_rows, precision=PRECISE))
    local_terms = jnp.concatenate(blocks, axis=1) / S
    coupling = lax.psum(local_terms, "tm").reshape(frames - 1, frames, rank_cols, rank_cols)
    shifted = jnp.concatenate(
        [jnp.zeros((1, frames, rank_cols, rank_cols), jnp.float32), coupling], axis=0
    )

    def solve_back(turn_index, response):
        column = frames - 1 - turn_index
        factors = lax.dynamic_index_in_dim(shifted, column, 1, keepdims=False)
        coupled = jnp.einsum("kab,kaw->bw", factors, response, precision=PRECISE)
        own_rows = lax.dynamic_index_in_dim(vb_rows, column, 0, keepdims=False)
        return lax.dynamic_update_index_in_dim(response, own_rows + coupled, column, 0)

    response = lax.fori_loop(
        0, frames, solve_back, jnp.zeros((frames, rank_cols, cells), jnp.float32)
    )
    return (probes, final_reach, response)


def per_device(symbols, emission, decay, left_factor, right_factor, initial):
    decay_row = decay[0]
    left_rows = left_factor[0]
    right_rows = right_factor[0]
    onehot = (symbols[:, None] == jnp.arange(emission.shape[1], dtype=jnp.int32)[None, :]).astype(
        jnp.float32
    )
    emitted_all = jnp.einsum("fv,sv->fs", onehot, emission, precision=PRECISE)
    leader = lax.axis_index("state") == 0

    def pass_on(closing):
        return jnp.where(leader, initial, passed_along(closing, "state", 1))

    probes, final_reach, response = span_map(emitted_all, decay_row, left_rows, right_rows)
    frames = emitted_all.shape[0]
    rank_cols = left_rows.shape[0]

    def section(step_idx, entry_vec):
        projected, total_sum = lax.psum(
            (jnp.dot(probes, entry_vec, precision=PRECISE), jnp.sum(entry_vec)), "tm"
        )
        rescale = S / total_sum
        carried = jnp.einsum(
            "ka,kaw->w",
            (projected * rescale).reshape(frames, rank_cols),
            response,
            precision=PRECISE,
        )
        return pass_on(final_reach * entry_vec * rescale + carried)

    entry_vec = lax.fori_loop(0, lax.axis_size("state") - 1, section, initial)
    beliefs, log_levels, closing = run_span(
        entry_vec, emitted_all, decay_row, left_rows, right_rows
    )
    return (beliefs, log_levels)


def solution(mesh):
    return jax.shard_map(
        per_device,
        mesh=mesh,
        in_specs=(
            P("state"),
            P("tm", None),
            P("state", "tm"),
            P("state", None, "tm"),
            P("state", None, "tm"),
            P("tm"),
        ),
        out_specs=(P("state", "tm"), P("state")),
        check_vma=False,
    )
```

profile of v0, /device:TPU:0, one launch (start us, length us, event | category | flops | bytes accessed | tf_op | source)
XLA Modules:
  0.0 347.2 jit_solution(12387997942848952314)
XLA Ops:
  7.3 0.9 slice_bitcast_fusion
  8.2 0.1 copy-done
  8.3 0.6 copy-done.3
  8.9 0.4 broadcast_multiply_fusion.10
  9.3 0.8 while.54
  9.3 0.1 bitcast_dynamic-update-slice_fusion.2
  9.5 0.1 bitcast_dynamic-update-slice_fusion.2
  9.7 0.1 bitcast_dynamic-update-slice_fusion.2
  9.9 0.1 bitcast_dynamic-update-slice_fusion.2
  10.1 0.1 copy-done.2
  10.2 1.1 broadcast_multiply_fusion
  11.3 1.0 convolution_dynamic-update-slice_fusion.7
  12.2 1.0 convolution_dynamic-update-slice_fusion.6
  13.2 1.0 convolution_dynamic-update-slice_fusion.5
  14.2 1.0 convolution_dynamic-update-slice_fusion.4
  15.2 1.0 convolution_dynamic-update-slice_fusion.3
  16.1 1.0 convolution_dynamic-update-slice_fusion.2
  17.1 1.0 convolution_dynamic-update-slice_fusion.1
  18.1 1.0 convolution_dynamic-update-slice_fusion
  19.1 0.2 reshape.155
  19.3 0.9 copy.8
  20.2 0.9 copy-done.1
  21.2 0.6 copy-done.4
  21.8 0.6 reduce_sum.28
  22.4 0.5 fusion.17
  22.9 44.2 %all-reduce.3 = (f32[256]{0:T(256)S(1)}, f32[]{:T(128)}) all-reduce(f32[256]{0:T(256)S(1)} %bitcast.161, f32[]{:T(128)} %reduce_sum.28), channel_id=1, replica_groups=mesh['tm'=16,'state'=2] {'tm'}, use_global_device_ids=true, to_apply=%region_4.5 | all-reduce | flops 257 | bytes 2056 | tf_op jit(solution)/shard_map/while/body/eval_jaxpr/psum | solution.py:109
  67.7 0.1 reshape.163
  67.8 0.1 broadcast_multiply_fusion.8
  67.9 63.9 %all-reduce.8.cloned.1.call-done = f32[3,4,64,64]{2,3,0,1:T(8,128)} async-done(((f32[3,4,64,64]{2,3,0,1:T(8,128)}), f32[3,4,64,64]{2,3,0,1:T(8,128)}) %all-reduce.8.cloned.1.call-update) | async-done | bytes 196624 | tf_op jit(solution)/shard_map/psum | solution.py:73
  131.8 1.0 concatenate.7
  132.9 2.0 while.52
  133.0 0.5 fusion.58
  133.4 0.4 fusion.58
  133.9 0.5 fusion.58
  134.4 0.4 fusion.58
  134.9 0.4 fusion.18
  135.3 1.3 collective-permute-start
  136.6 0.8 collective-permute-done
  137.4 0.6 fusion.16
  138.0 0.2 convolution_bitcast_fusion.2
  138.2 40.5 %all-reduce.2 = (f32[]{:T(128)}, f32[64]{0:T(128)S(1)}) all-reduce(f32[]{:T(128)} %get-tuple-element.314, f32[64]{0:T(128)S(1)} %convolution_bitcast_fusion.2), channel_id=1, replica_groups=mesh['tm'=16,'state'=2] {'tm'}, use_global_device_ids=true, to_apply=%region_9.10 | all-reduce | flops 65 | bytes 520 | tf_op jit(solution)/shard_map/psum | solution.py:19
  179.4 160.4 %while.53 = (s32[]{:T(128)}, f32[512]{0:T(512)S(1)}, f32[64]{0:T(128)S(1)}, f32[4,512]{1,0:T(4,128)S(1)}, f32[4]{0:T(128)S(1)}, /*index=5*/f32[4,512]{1,0:T(4,12...) while((s32[]{:T(128)}, f32[512]{0:T(512)S(1)}, ...), condition=%wide.region_15.16_spmd, body=%wide.region_11.15_spmd.sunk | while | flops 789187 | bytes 290481 | solution.py:39
  179.4 0.2 fusion.63
  179.6 0.6 fusion.64
  180.2 0.2 convolution_bitcast_fusion.4
  180.4 37.2 %all-reduce.5 = (f32[]{:T(128)}, f32[64]{0:T(128)S(1)}) all-reduce(f32[]{:T(128)} %get-tuple-element.468, f32[64]{0:T(128)S(1)} %convolution_bitcast_fusion.4), channel_id=1, replica_groups=mesh['tm'=16,'state'=2] {'tm'}, use_global_device_ids=true, to_apply=%region_13.13 | all-reduce | flops 65 | bytes 520 | tf_op jit(solution)/shard_map/while/body/eval_jaxpr/psum | solution.py:31
  218.4 0.1 dynamic_update_slice.37
  218.5 0.2 fusion.63
  218.7 0.6 fusion.64
  219.3 0.2 convolution_bitcast_fusion.4
  219.5 39.2 %all-reduce.5 = (f32[]{:T(128)}, f32[64]{0:T(128)S(1)}) all-reduce(f32[]{:T(128)} %get-tuple-element.468, f32[64]{0:T(128)S(1)} %convolution_bitcast_fusion.4), channel_id=1, replica_groups=mesh['tm'=16,'state'=2] {'tm'}, use_global_device_ids=true, to_apply=%region_13.13 | all-reduce | flops 65 | bytes 520 | tf_op jit(solution)/shard_map/while/body/eval_jaxpr/psum | solution.py:31
  259.5 0.1 dynamic_update_slice.37
  259.6 0.2 fusion.63
  259.8 0.6 fusion.64
  260.4 0.2 convolution_bitcast_fusion.4
  260.5 37.3 %all-reduce.5 = (f32[]{:T(128)}, f32[64]{0:T(128)S(1)}) all-reduce(f32[]{:T(128)} %get-tuple-element.468, f32[64]{0:T(128)S(1)} %convolution_bitcast_fusion.4), channel_id=1, replica_groups=mesh['tm'=16,'state'=2] {'tm'}, use_global_device_ids=true, to_apply=%region_13.13 | all-reduce | flops 65 | bytes 520 | tf_op jit(solution)/shard_map/while/body/eval_jaxpr/psum | solution.py:31
  298.6 0.1 dynamic_update_slice.37
  298.7 0.2 fusion.63
  298.9 0.6 fusion.64
  299.5 0.2 convolution_bitcast_fusion.4
  299.7 39.2 %all-reduce.5 = (f32[]{:T(128)}, f32[64]{0:T(128)S(1)}) all-reduce(f32[]{:T(128)} %get-tuple-element.468, f32[64]{0:T(128)S(1)} %convolution_bitcast_fusion.4), channel_id=1, replica_groups=mesh['tm'=16,'state'=2] {'tm'}, use_global_device_ids=true, to_apply=%region_13.13 | all-reduce | flops 65 | bytes 520 | tf_op jit(solution)/shard_map/while/body/eval_jaxpr/psum | solution.py:31
  339.7 0.1 dynamic_update_slice.37
  339.8 0.5 copy-done.7
  340.3 0.1 copy-done.5
  (63 shorter events, 0.9 us)
Async XLA Ops:
  7.2 1.2 copy-start
  7.2 124.7 %all-reduce.8.cloned.1.call-start = ((), (), s32[]{:S(2)}) async-start(), calls=%async_computation | async-start | bytes 786432 | tf_op jit(solution)/shard_map/psum | solution.py:73
  8.2 0.7 copy-start.3
  8.2 0.7 copy-start.6
  9.2 0.9 copy-start.2
  20.2 0.9 copy-start.1
  21.1 0.7 copy-start.4
  135.3 2.1 collective-permute-start
  339.8 0.5 copy-start.7
  339.8 0.6 copy-start.5
Sparse Core Ops, SparseCore 0:
  20.3 111.4 all-reduce.7
where the time goes:
time: 348 us; the launch traced here: 347 us
  blocking collectives  238 us (68%)
  waiting for transfers between devices  64.7 us (19%)
  between operations  15.6 us (4%)
  matrix products  12.4 us (4%)
  local copies, waits for them, and re-layouts  7.07 us (2%)
  other arithmetic  5.31 us (2%)
    psum x4, blocking collectives, frame(): lax.psum((jnp.dot(left_rows, unscaled, precision=PRECISE), jnp.sum(unscal...  153 us
    psum x1, waiting for transfers between devices, span_map(): lax.psum(local_terms, 'tm')  63.9 us
    psum x1, blocking collectives, section(): lax.psum((jnp.dot(probes, entry_vec, precision=PRECISE), jnp.sum(entry_ve...  44.2 us
    psum x1, blocking collectives, run_span(): lax.psum((jnp.dot(left_rows, entry_vec, precision=PRECISE), jnp.sum(entry...  40.5 us
    dot_general x8, matrix products, span_map(): jnp.einsum('pw,qw->pq', pair_rows, cross_rows, precision=PRECISE)  7.79 us
  transfers between devices with their start and end apart: 2, of which 2 were waited for; matrix products, arithmetic and copies ran while one was open for 0% of the time, Pallas kernels for 0%

commit v1 on v0

v1 whole, which is shorter than its diff:
```python
import functools

import jax
import jax.numpy as jnp
from jax import lax
from jax.experimental import pallas as pl
from jax.experimental.pallas import tpu as pltpu
from jax.sharding import PartitionSpec as P

F32 = jnp.float32
BF16 = jnp.bfloat16
ROWS = 8


def split(x):
    hi = x.astype(BF16)
    return hi, (x - hi.astype(F32)).astype(BF16)


def stacked(x):
    hi = x.astype(BF16).astype(F32)
    return jnp.concatenate([hi, x - hi], axis=0).astype(BF16)


def dot2(x, pieces, dims):
    both = stacked(x)
    total = sum(
        lax.dot_general(both, piece, (dims, ((), ())), preferred_element_type=F32)
        for piece in pieces
    )
    return total[: x.shape[0]] + total[x.shape[0] :]


ALONG = ((1,), (1,))
ACROSS = ((1,), (0,))


def kernel(
    tiles,
    spans,
    symbols,
    emission_hbm,
    decay_hbm,
    left_hbm,
    right_hbm,
    initial_hbm,
    beliefs_out,
    logs_out,
    emission,
    decay,
    left,
    right,
    entry,
    closing,
    side,
    kbuf,
    rbuf,
    gown,
    gbuf,
    kfull,
    pbuf,
    pall,
    load_sem,
    rs_send,
    rs_recv,
    ag_send,
    ag_recv,
    p_send,
    p_recv,
    pass_send,
    pass_recv,
):
    me = lax.axis_index("tm")
    span = lax.axis_index("state")
    frames = beliefs_out.shape[0]
    rank, cells = right.shape
    width = kfull.shape[1]
    share = rank // tiles
    states = cells * tiles
    pairs = [(t, s) for s in range(frames) for t in range(s + 1, frames)]
    sums = [(t, s) for s in range(frames) for t in range(s + 1, frames + 1)]

    barrier = pltpu.get_barrier_semaphore()
    peers = [lax.rem(me + k, tiles) for k in range(tiles)]
    for k in range(1, tiles):
        pl.semaphore_signal(barrier, inc=1, device_id={"tm": peers[k]})
    turns = sorted({1 % spans, (spans - 1) % spans} - {0})
    for k in turns:
        pl.semaphore_signal(barrier, inc=1, device_id={"state": lax.rem(span + k, spans)})

    loads = [
        pltpu.make_async_copy(src, dst, load_sem.at[i])
        for i, (src, dst) in enumerate(
            (
                (emission_hbm, emission),
                (decay_hbm, decay),
                (left_hbm.at[0], left),
                (right_hbm.at[0], right),
            )
        )
    ]
    for load in loads:
        load.start()

    @pl.when(span == 0)
    def _():
        copy = pltpu.make_async_copy(initial_hbm, entry, load_sem.at[4])
        copy.start()
        copy.wait()

    row_id = lax.broadcasted_iota(jnp.int32, (ROWS, emission.shape[1]), 0)
    column_id = lax.broadcasted_iota(jnp.int32, (ROWS, emission.shape[1]), 1)
    wanted = jnp.full(row_id.shape, -1, jnp.int32)
    for t in range(frames):
        wanted = jnp.where(row_id == t, symbols[t], wanted)
    onehot = jnp.where(wanted == column_id, 1.0, 0.0).astype(BF16)
    for load in loads:
        load.wait()
    emitted = sum(
        lax.dot_general(onehot, piece, (ALONG, ((), ())), preferred_element_type=F32)
        for piece in split(emission[...])
    )
    emit = [emitted[t : t + 1] for t in range(frames)]
    grow = [emit[t] * decay[...] for t in range(frames)]
    scaled = left[...] * (1.0 / states)
    scaled_pieces = split(scaled)

    def send_projection():
        row = entry[...]
        rows = [row]
        for t in range(frames):
            row = row * grow[t]
            rows.append(row)
        rows += [jnp.zeros_like(row)] * (ROWS - len(rows))
        reached = jnp.concatenate(rows, axis=0)
        pbuf[:, :rank] = dot2(reached, scaled_pieces, ALONG)
        pbuf[:, rank:] = jnp.broadcast_to(
            jnp.sum(reached, axis=1, keepdims=True), (ROWS, pbuf.shape[1] - rank)
        )
        for k in range(1, tiles):
            p_copy(k).start()

    def p_copy(k):
        return pltpu.make_async_remote_copy(
            pbuf, pall.at[k - 1], p_send.at[k - 1], p_recv.at[k - 1], device_id={"tm": peers[k]}
        )

    def rs_copy(k):
        return pltpu.make_async_remote_copy(
            kbuf.at[peers[k]],
            rbuf.at[k - 1],
            rs_send.at[k - 1],
            rs_recv.at[k - 1],
            device_id={"tm": peers[k]},
        )

    def ag_copy(k):
        return pltpu.make_async_remote_copy(
            gown, gbuf.at[me], ag_send.at[k - 1], ag_recv.at[k - 1], device_id={"tm": peers[k]}
        )

    def pass_copy():
        return pltpu.make_async_remote_copy(
            closing, entry, pass_send, pass_recv, device_id={"state": lax.rem(span + 1, spans)}
        )

    reach = {}
    for s in range(frames):
        weight = emit[s]
        reach[s + 1, s] = weight
        for t in range(s + 1, frames):
            weight = weight * grow[t]
            reach[t + 1, s] = weight
    for i, pair in enumerate(pairs):
        side[i * rank : (i + 1) * rank] = reach[pair] * scaled
    base = len(pairs) * rank
    side[base:] = jnp.zeros((width - base, cells), F32)
    for i, pair in enumerate(sums):
        side[base + i : base + i + 1] = reach[pair]

    coupling = dot2(right[...], split(side[...]), ALONG)
    for j in range(tiles):
        kbuf[j] = coupling[j * share : (j + 1) * share]

    pl.semaphore_wait(barrier, tiles - 1 + len(turns))

    @pl.when(span == 0)
    def _():
        send_projection()

    for k in range(1, tiles):
        rs_copy(k).start()
    total = kbuf[me]
    for k in range(1, tiles):
        rs_copy(k).wait_recv()
        total = total + rbuf[k - 1]
    gown[...] = total
    for k in range(1, tiles):
        ag_copy(k).start()
    gbuf[me] = total
    for k in range(1, tiles):
        ag_copy(k).wait_recv()
    for j in range(tiles):
        kfull[j * share : (j + 1) * share] = gbuf[j]
    matrices = {
        pair: split(kfull[:, i * rank : (i + 1) * rank]) for i, pair in enumerate(pairs)
    }
    sum_matrix = split(kfull[:, base:])

    @pl.when(span > 0)
    def _():
        pass_copy().wait_recv()
        send_projection()

    projected = pbuf[...]
    for k in range(1, tiles):
        p_copy(k).wait_recv()
        projected = projected + pall[k - 1]
    mix = projected[:, :rank]
    mix_row = lax.broadcasted_iota(jnp.int32, mix.shape, 0)
    mix = jnp.where(mix_row < frames, mix, 0.0)
    for s in range(frames - 1):
        for t in range(s + 1, frames):
            term = dot2(mix, matrices[t, s], ACROSS)[s : s + 1]
            mix = mix + jnp.where(mix_row == t, term, 0.0)
    lifted = dot2(mix, split(right[...]), ACROSS)
    belief = entry[...]
    kept = []
    for t in range(frames):
        belief = grow[t] * belief + emit[t] * lifted[t : t + 1]
        kept.append(belief)
    if spans > 1:
        closing[...] = belief

        @pl.when(span < spans - 1)
        def _():
            pass_copy().start()

    parts = dot2(mix, sum_matrix, ACROSS)
    part_row = lax.broadcasted_iota(jnp.int32, parts.shape, 0)
    part_column = lax.broadcasted_iota(jnp.int32, parts.shape, 1)
    mass = [projected[0:1, rank : rank + 1]]
    for t in range(1, frames + 1):
        hit = jnp.zeros(parts.shape, jnp.bool_)
        for i, (u, s) in enumerate(sums):
            if u == t:
                hit = hit | ((part_row == s) & (part_column == i))
        mass.append(
            projected[t : t + 1, rank : rank + 1]
            + jnp.sum(jnp.where(hit, parts, 0.0), keepdims=True)
        )
    lane = lax.broadcasted_iota(jnp.int32, logs_out.shape, 1)
    logs = jnp.zeros(logs_out.shape, F32)
    for t in range(frames):
        beliefs_out[t : t + 1] = kept[t] * (states / mass[t + 1])
        logs = jnp.where(lane == t, mass[t + 1] / mass[t], logs)
    logs_out[...] = jnp.log(jnp.where(lane < frames, logs, 1.0))

    for k in range(1, tiles):
        p_copy(k).wait_send()
        rs_copy(k).wait_send()
        ag_copy(k).wait_send()
    if spans > 1:

        @pl.when(span < spans - 1)
        def _():
            pass_copy().wait_send()


def solution(mesh):
    tiles, spans = mesh.shape["tm"], mesh.shape["state"]

    def per_device(symbols, emission, decay, left_factor, right_factor, initial):
        frames = symbols.shape[0]
        rank, cells = left_factor.shape[1:]
        pair_count = frames * (frames - 1) // 2
        sum_count = frames * (frames + 1) // 2
        width = -(-(pair_count * rank + sum_count) // 128) * 128
        share = rank // tiles
        vmem, dma = pltpu.VMEM, pltpu.SemaphoreType.DMA
        others = tiles - 1
        beliefs, logs = pl.pallas_call(
            functools.partial(kernel, tiles, spans),
            out_shape=(
                jax.ShapeDtypeStruct((frames, cells), F32),
                jax.ShapeDtypeStruct((1, 128), F32),
            ),
            in_specs=[pl.BlockSpec(memory_space=pltpu.SMEM)]
            + [pl.BlockSpec(memory_space=pl.ANY)] * 5,
            out_specs=(pl.BlockSpec(memory_space=vmem),) * 2,
            scratch_shapes=[
                vmem(emission.shape, F32),
                vmem(decay.shape, F32),
                vmem((rank, cells), F32),
                vmem((rank, cells), F32),
                vmem((1, cells), F32),
                vmem((1, cells), F32),
                vmem((width, cells), F32),
                vmem((tiles, share, width), F32),
                vmem((others, share, width), F32),
                vmem((share, width), F32),
                vmem((tiles, share, width), F32),
                vmem((rank, width), F32),
                vmem((ROWS, 128), F32),
                vmem((others, ROWS, 128), F32),
                dma((5,)),
                dma((others,)),
                dma((others,)),
                dma((others,)),
                dma((others,)),
                dma((others,)),
                dma((others,)),
                dma(()),
                dma(()),
            ],
            compiler_params=pltpu.CompilerParams(collective_id=0, has_side_effects=True),
        )(symbols, emission, decay, left_factor, right_factor, initial.reshape(1, cells))
        return beliefs, logs[0, :frames]

    return jax.shard_map(
        per_device,
        mesh=mesh,
        in_specs=(
            P("state"),
            P("tm", None),
            P("state", "tm"),
            P("state", None, "tm"),
            P("state", None, "tm"),
            P("tm"),
        ),
        out_specs=(P("state", "tm"), P("state")),
        check_vma=False,
    )
```

time: 348 us -> 29.2 us (0.08)
  the two profiles are of different devices: /device:TPU:0 before, /device:TPU:1 now
where the time goes in v1:
time: 29.2 us; the launch traced here: 29 us
  Pallas kernels  25.9 us (89%)
  local copies, waits for them, and re-layouts  2.47 us (8%)
  between operations  0.65 us (2%)
    pallas_call x1, Pallas kernels, per_device(): pl.pallas_call(functools.partial(kernel, tiles, spans), out_shape=(jax.Sh...  25.9 us
    unnamed x3, local copies, waits for them, and re-layouts  1.95 us

profile of v1, /device:TPU:1, one launch (start us, length us, event | category | flops | bytes accessed | tf_op | source)
XLA Modules:
  0.0 29.0 jit_solution(15524082639155224733)
XLA Ops:
  0.6 25.9 %shard_map.77 = (f32[4,512]{1,0:T(4,128)}, f32[1,128]{1,0:T(1,128)}) custom-call(s32[4]{0:T(128)} %symbols.1, f32[512,256]{1,0:T(8,128)} %emission_hbm.1, f32[1,512]{1,0:T(1,128)} %decay_hbm.1, f32[1,64,512]{2,1,0:T(8,128)} %left_hbm.1, f32[1,64,512]{2,1,0:T(8,128)} %right_hbm.1, f32[1,512]{1,0:T(1,128)} %bitcast.3), custom_call_target="tpu_custom_call" | custom-call | tf_op jit(solution)/shard_map/pallas_call | solution.py:282
  26.5 0.0 copy-start
  26.5 0.7 %copy-done = f32[1,128]{1,0:T(1,128)S(1)} copy-done((f32[1,128]{1,0:T(1,128)S(1)}, f32[1,128]{1,0:T(1,128)}, u32[]{:S(2)}) %copy-start) | copy-done | bytes 536
  27.2 0.5 %slice_bitcast_fusion = f32[4]{0:T(128)} fusion(f32[1,128]{1,0:T(1,128)S(1)} %copy-done), kind=kLoop, calls=%fused_computation | loop fusion | bytes 32 | tf_op jit(solution)/shard_map/squeeze | solution.py:318
  27.7 1.3 %copy.9 = f32[4,512]{1,0:T(4,128)} copy(f32[4,512]{1,0:T(4,128)} %get-tuple-element.8) | data formatting | bytes 16384
Async XLA Ops:
  26.5 0.7 %copy-start = (f32[1,128]{1,0:T(1,128)S(1)}, f32[1,128]{1,0:T(1,128)}, u32[]{:S(2)}) copy-start(f32[1,128]{1,0:T(1,128)} %get-tuple-element.5) | copy-start | bytes 1540

commit v2 on v1

--- a/solution.py
+++ b/solution.py
@@ -44,8 +44,7 @@
     left_hbm,
     right_hbm,
     initial_hbm,
-    beliefs_out,
-    logs_out,
+    packed,
     emission,
     decay,
     left,
@@ -72,7 +71,7 @@
 ):
     me = lax.axis_index("tm")
     span = lax.axis_index("state")
-    frames = beliefs_out.shape[0]
+    frames = symbols.shape[0]
     rank, cells = right.shape
     width = kfull.shape[1]
     share = rank // tiles
@@ -249,12 +248,12 @@
             projected[t : t + 1, rank : rank + 1]
             + jnp.sum(jnp.where(hit, parts, 0.0), keepdims=True)
         )
-    lane = lax.broadcasted_iota(jnp.int32, logs_out.shape, 1)
-    logs = jnp.zeros(logs_out.shape, F32)
+    lane = lax.broadcasted_iota(jnp.int32, (1, 128), 1)
+    levels = jnp.ones(lane.shape, F32)
     for t in range(frames):
-        beliefs_out[t : t + 1] = kept[t] * (states / mass[t + 1])
-        logs = jnp.where(lane == t, mass[t + 1] / mass[t], logs)
-    logs_out[...] = jnp.log(jnp.where(lane < frames, logs, 1.0))
+        packed[t : t + 1] = kept[t] * (states / mass[t + 1])
+        levels = jnp.where(lane == t, mass[t + 1] / mass[t], levels)
+    packed[frames : frames + 1, :128] = jnp.log(levels)
 
     for k in range(1, tiles):
         p_copy(k).wait_send()
@@ -265,6 +264,12 @@
         @pl.when(span < spans - 1)
         def _():
             pass_copy().wait_send()
+
+
+def unpack(packed, beliefs_out, logs_out):
+    frames = beliefs_out.shape[0]
+    beliefs_out[...] = packed[:frames]
+    logs_out[...] = packed[frames, :frames]
 
 
 def solution(mesh):
@@ -279,15 +284,12 @@
         share = rank // tiles
         vmem, dma = pltpu.VMEM, pltpu.SemaphoreType.DMA
         others = tiles - 1
-        beliefs, logs = pl.pallas_call(
+        packed = pl.pallas_call(
             functools.partial(kernel, tiles, spans),
-            out_shape=(
-                jax.ShapeDtypeStruct((frames, cells), F32),
-                jax.ShapeDtypeStruct((1, 128), F32),
-            ),
+            out_shape=vmem((ROWS, cells), F32),
             in_specs=[pl.BlockSpec(memory_space=pltpu.SMEM)]
-            + [pl.BlockSpec(memory_space=pl.ANY)] * 5,
-            out_specs=(pl.BlockSpec(memory_space=vmem),) * 2,
+            + [pl.BlockSpec(memory_space=pltpu.HBM)] * 5,
+            out_specs=pl.BlockSpec(memory_space=vmem),
             scratch_shapes=[
                 vmem(emission.shape, F32),
                 vmem(decay.shape, F32),
@@ -315,7 +317,16 @@
             ],
             compiler_params=pltpu.CompilerParams(collective_id=0, has_side_effects=True),
         )(symbols, emission, decay, left_factor, right_factor, initial.reshape(1, cells))
-        return beliefs, logs[0, :frames]
+        return pl.pallas_call(
+            unpack,
+            out_shape=(
+                jax.ShapeDtypeStruct((frames, cells), F32),
+                jax.ShapeDtypeStruct((frames,), F32),
+            ),
+            in_specs=[pl.BlockSpec(memory_space=vmem)],
+            out_specs=(pl.BlockSpec(memory_space=vmem),) * 2,
+            compiler_params=pltpu.CompilerParams(vmem_limit_bytes=16 * 2**20),
+        )(packed)
 
     return jax.shard_map(
         per_device,

time: 29.2 us -> 26.7 us (0.914)
  local copies, waits for them, and re-layouts: 2.47 us -> 0 us
    unnamed x3 -> x0, local copies, waits for them, and re-layouts: 1.95 us -> none
    squeeze x1 -> x0, local copies, waits for them, and re-layouts: 0.51 us -> none  [per_device(): return (beliefs, logs[0, :frames])]
    pallas_call x1 -> x2, Pallas kernels: 25.9 us -> 25.9 us  [the longest x1 25.3 us: per_device(): pl.pallas_call(functools.partial(kernel, tiles, spans), out_shape=vmem((R...]
where the time goes in v2:
time: 26.7 us; the launch traced here: 26.5 us
  Pallas kernels  25.9 us (97%)
  between operations  0.64 us (2%)
    pallas_call x1, Pallas kernels, per_device(): pl.pallas_call(functools.partial(kernel, tiles, spans), out_shape=vmem((R...  25.3 us
    pallas_call x1, Pallas kernels, per_device(): pl.pallas_call(unpack, out_shape=(jax.ShapeDtypeStruct((frames, cells), F...  0.6 us

profile of v2, /device:TPU:1, one launch (start us, length us, event | category | flops | bytes accessed | tf_op | source)
XLA Modules:
  0.0 26.5 jit_solution(16343873190499075666)
XLA Ops:
  0.6 25.3 %shard_map.77.packed = f32[8,512]{1,0:T(8,128)S(1)} custom-call(s32[4]{0:T(128)} %symbols.1, f32[512,256]{1,0:T(8,128)} %emission_hbm.1, f32[1,512]{1,0:T(1,128)} %decay_hbm.1, f32[1,64,512]{2,1,0:T(8,128)} %left_hbm.1, f32[1,64,512]{2,1,0:T(8,128)} %right_hbm.1, f32[1,512]{1,0:T(1,128)} %bitcast.1), custom_call_target="tpu_custom_call" | custom-call | tf_op jit(solution)/shard_map/pallas_call | solution.py:287
  25.9 0.6 %shard_map.78 = (f32[4,512]{1,0:T(4,128)}, f32[4]{0:T(128)}) custom-call(f32[8,512]{1,0:T(8,128)S(1)} %shard_map.77.packed), custom_call_target="tpu_custom_call" | custom-call | tf_op jit(solution)/shard_map/pallas_call | solution.py:320

commit v3 on v2

v3 whole, which is shorter than its diff:
```python
import functools

import jax
import jax.numpy as jnp
from jax import lax
from jax.experimental import pallas as pl
from jax.experimental.pallas import tpu as pltpu
from jax.sharding import PartitionSpec as P

F32 = jnp.float32
BF16 = jnp.bfloat16
ROWS = 8


def split(x):
    hi = x.astype(BF16)
    return hi, (x - hi.astype(F32)).astype(BF16)


def stacked(x):
    hi = x.astype(BF16).astype(F32)
    return jnp.concatenate([hi, x - hi], axis=0).astype(BF16)


def dot2(x, pieces, dims):
    both = stacked(x)
    total = sum(
        lax.dot_general(both, piece, (dims, ((), ())), preferred_element_type=F32)
        for piece in pieces
    )
    return total[: x.shape[0]] + total[x.shape[0] :]


ALONG = ((1,), (1,))
ACROSS = ((1,), (0,))
LAST = 1


def kernel(
    tiles,
    symbols,
    emission_hbm,
    decay_hbm,
    left_hbm,
    right_hbm,
    initial_hbm,
    packed,
    emission,
    decay,
    left,
    right,
    entry,
    side,
    first_pieces,
    first_parts,
    first_own,
    first_all,
    first_full,
    last_pieces,
    last_parts,
    last_own,
    last_all,
    last_full,
    pbuf,
    first_proj,
    last_proj,
    pace,
    first_pace,
    first_right,
    hand,
    handed,
    mass_out,
    mass_in,
    load_sem,
    fs_send,
    fs_recv,
    fg_send,
    fg_recv,
    ls_send,
    ls_recv,
    lg_send,
    lg_recv,
    fp_send,
    fp_recv,
    lp_send,
    lp_recv,
    chip_send,
    chip_recv,
    clear,
):
    me = lax.axis_index("tm")
    span = lax.axis_index("state")
    frames = symbols.shape[0]
    rank, cells = right.shape
    share = rank // tiles
    states = cells * tiles
    pairs = [(t, s) for s in range(frames) for t in range(s + 1, frames)]
    sums = [(t, s) for s in range(frames) for t in range(s + 1, frames + 1)]
    base = len(pairs) * rank
    width = last_full.shape[1]
    peers = [lax.rem(me + k, tiles) for k in range(tiles)]
    half = rank + 32

    barrier = pltpu.get_barrier_semaphore()

    @pl.when(span < LAST)
    def _():
        for k in range(tiles):
            pl.semaphore_signal(barrier, inc=1, device_id={"tm": peers[k], "state": LAST})

    @pl.when(span == LAST)
    def _():
        for k in range(1, tiles):
            pl.semaphore_signal(barrier, inc=1, device_id={"tm": peers[k], "state": LAST})
        for k in range(tiles):
            pl.semaphore_signal(barrier, inc=1, device_id={"tm": peers[k], "state": 0})

    loads = [
        pltpu.make_async_copy(src, dst, load_sem.at[i])
        for i, (src, dst) in enumerate(
            (
                (emission_hbm, emission),
                (decay_hbm, decay),
                (left_hbm.at[0], left),
                (right_hbm.at[0], right),
                (initial_hbm, entry),
            )
        )
    ]
    for load in loads:
        load.start()

    def remote(src, dst, send, recv, tile, state):
        return pltpu.make_async_remote_copy(
            src, dst, send, recv, device_id={"tm": tile, "state": state}
        )

    def first_scatter(k):
        return remote(
            first_pieces.at[peers[k]], first_parts.at[k], fs_send.at[k], fs_recv.at[k], peers[k], LAST
        )

    def first_project(k):
        return remote(pbuf, first_proj.at[k], fp_send.at[k], fp_recv.at[k], peers[k], LAST)

    def first_gather(k):
        return remote(
            first_own, first_all.at[me], fg_send.at[k - 1], fg_recv.at[k - 1], peers[k], LAST
        )

    def last_scatter(k):
        return remote(
            last_pieces.at[peers[k]],
            last_parts.at[k - 1],
            ls_send.at[k - 1],
            ls_recv.at[k - 1],
            peers[k],
            LAST,
        )

    def last_gather(k):
        return remote(
            last_own, last_all.at[me], lg_send.at[k - 1], lg_recv.at[k - 1], peers[k], LAST
        )

    def last_project(k):
        return remote(
            pbuf, last_proj.at[k - 1], lp_send.at[k - 1], lp_recv.at[k - 1], peers[k], LAST
        )

    def give(i):
        src, dst, state = (
            (right, first_right, LAST),
            (pace, first_pace, LAST),
            (hand, handed, 0),
            (mass_out, mass_in, 0),
        )[i]
        return remote(src, dst, chip_send.at[i], chip_recv.at[i], me, state)

    row_id = lax.broadcasted_iota(jnp.int32, (ROWS, emission.shape[1]), 0)
    column_id = lax.broadcasted_iota(jnp.int32, (ROWS, emission.shape[1]), 1)
    wanted = jnp.full(row_id.shape, -1, jnp.int32)
    for t in range(frames):
        wanted = jnp.where(row_id == t, symbols[t], wanted)
    onehot = jnp.where(wanted == column_id, 1.0, 0.0).astype(BF16)
    for load in loads:
        load.wait()
    emitted = sum(
        lax.dot_general(onehot, piece, (ALONG, ((), ())), preferred_element_type=F32)
        for piece in split(emission[...])
    )
    emit = [emitted[t : t + 1] for t in range(frames)]
    grow = [emit[t] * decay[...] for t in range(frames)]
    scaled = left[...] * (1.0 / states)
    scaled_pieces = split(scaled)
    for t in range(frames):
        pace[t : t + 1] = emit[t]
        pace[frames + t : frames + t + 1] = grow[t]

    def projections(row):
        rows = [row]
        for t in range(frames):
            row = row * grow[t]
            rows.append(row)
        rows += [jnp.zeros_like(row)] * (ROWS - len(rows))
        reached = jnp.concatenate(rows, axis=0)
        pbuf[:, :rank] = dot2(reached, scaled_pieces, ALONG)
        pbuf[:, rank:half] = jnp.broadcast_to(
            jnp.sum(reached, axis=1, keepdims=True), (ROWS, half - rank)
        )

    def couplings():
        reach = {}
        for s in range(frames):
            weight = emit[s]
            reach[s + 1, s] = weight
            for t in range(s + 1, frames):
                weight = weight * grow[t]
                reach[t + 1, s] = weight
        for i, pair in enumerate(pairs):
            side[i * rank : (i + 1) * rank] = reach[pair] * scaled
        side[base:] = jnp.zeros((width - base, cells), F32)
        for i, pair in enumerate(sums):
            side[base + i : base + i + 1] = reach[pair]
        return dot2(right[...], split(side[...]), ALONG)

    def solve(mix, full):
        mix_row = lax.broadcasted_iota(jnp.int32, mix.shape, 0)
        mix = jnp.where(mix_row < frames, mix, 0.0)
        for s in range(frames - 1):
            for i, (t, u) in enumerate(pairs):
                if u == s:
                    matrix = split(full[:, i * rank : (i + 1) * rank])
                    term = dot2(mix, matrix, ACROSS)[s : s + 1]
                    mix = mix + jnp.where(mix_row == t, term, 0.0)
        return mix

    def advance(belief, emits, grows, lifted):
        kept = []
        for t in range(frames):
            belief = grows[t] * belief + emits[t] * lifted[t : t + 1]
            kept.append(belief)
        return kept

    def write(kept, mass):
        lane = lax.broadcasted_iota(jnp.int32, (1, 128), 1)
        levels = jnp.ones(lane.shape, F32)
        for t in range(frames):
            packed[t : t + 1] = kept[t] * (states / mass[t + 1])
            levels = jnp.where(lane == t, mass[t + 1] / mass[t], levels)
        packed[frames : frames + 1, :128] = jnp.log(levels)

    coupling = couplings()

    @pl.when(span < LAST)
    def _():
        for j in range(tiles):
            first_pieces[j] = coupling[j * share : (j + 1) * share, :base]
        projections(entry[...])
        pbuf[:, half:] = jnp.zeros((ROWS, pbuf.shape[1] - half), F32)
        pl.semaphore_wait(barrier, tiles)
        for k in range(tiles):
            first_scatter(k).start()
        for k in range(tiles):
            first_project(k).start()
        give(0).start()
        give(1).start()
        for k in range(tiles):
            first_scatter(k).wait_send()
        pl.semaphore_signal(clear, inc=1, device_id={"tm": me, "state": LAST})
        for k in range(tiles):
            first_project(k).wait_send()
        give(0).wait_send()
        give(1).wait_send()
        give(2).wait_recv()
        kept = [handed[t : t + 1] for t in range(frames)]
        mass = [handed[frames : frames + 1, :1]]
        give(3).wait_recv()
        mass += [mass_in[t : t + 1, half : half + 1] for t in range(frames - 1)]
        mass += [mass_in[0:1, rank : rank + 1]]
        write(kept, mass)

    @pl.when(span == LAST)
    def _():
        for j in range(tiles):
            last_pieces[j] = coupling[j * share : (j + 1) * share]
        pl.semaphore_wait(barrier, 2 * tiles - 1)
        pl.semaphore_wait(clear, 1)
        for k in range(1, tiles):
            last_scatter(k).start()
        total = jnp.zeros(first_own.shape, F32)
        for k in range(tiles):
            first_scatter(k).wait_recv()
            total = total + first_parts[k]
        first_own[...] = total
        for k in range(1, tiles):
            first_gather(k).start()
        first_all[me] = total
        total = last_pieces[me]
        for k in range(1, tiles):
            last_scatter(k).wait_recv()
            total = total + last_parts[k - 1]
        last_own[...] = total
        for k in range(1, tiles):
            last_gather(k).start()
        last_all[me] = total

        projected = jnp.zeros(pbuf.shape, F32)
        for k in range(tiles):
            first_project(k).wait_recv()
            projected = projected + first_proj[k]
        give(0).wait_recv()
        give(1).wait_recv()
        for k in range(1, tiles):
            first_gather(k).wait_recv()
        for j in range(tiles):
            first_full[j * share : (j + 1) * share] = first_all[j]
        mix = solve(projected[:, :rank], first_full)
        lifted = dot2(mix, split(first_right[...]), ACROSS)
        emits = [first_pace[t : t + 1] for t in range(frames)]
        grows = [first_pace[frames + t : frames + t + 1] for t in range(frames)]
        kept = advance(entry[...], emits, grows, lifted)
        belief = kept[-1]
        projections(belief)
        partial = jnp.concatenate(
            kept[:-1] + [jnp.zeros((ROWS + 1 - frames, cells), F32)], axis=0
        )
        pbuf[:, half:] = jnp.broadcast_to(
            jnp.sum(partial, axis=1, keepdims=True), (ROWS, pbuf.shape[1] - half)
        )
        for k in range(1, tiles):
            last_project(k).start()
        for t in range(frames):
            hand[t : t + 1] = kept[t]
        hand[frames : frames + 1] = jnp.broadcast_to(projected[0:1, rank : rank + 1], (1, cells))
        give(2).start()

        for k in range(1, tiles):
            last_gather(k).wait_recv()
        for j in range(tiles):
            last_full[j * share : (j + 1) * share] = last_all[j]
        projected = pbuf[...]
        for k in range(1, tiles):
            last_project(k).wait_recv()
            projected = projected + last_proj[k - 1]
        mass_out[...] = projected
        give(3).start()
        mix = solve(projected[:, :rank], last_full)
        lifted = dot2(mix, split(right[...]), ACROSS)
        kept = advance(belief, emit, grow, lifted)
        parts = dot2(mix, split(last_full[:, base:]), ACROSS)
        part_row = lax.broadcasted_iota(jnp.int32, parts.shape, 0)
        part_column = lax.broadcasted_iota(jnp.int32, parts.shape, 1)
        mass = [projected[0:1, rank : rank + 1]]
        for t in range(1, frames + 1):
            hit = jnp.zeros(parts.shape, jnp.bool_)
            for i, (u, s) in enumerate(sums):
                if u == t:
                    hit = hit | ((part_row == s) & (part_column == i))
            mass.append(
                projected[t : t + 1, rank : rank + 1]
                + jnp.sum(jnp.where(hit, parts, 0.0), keepdims=True)
            )
        write(kept, mass)
        for k in range(1, tiles):
            last_scatter(k).wait_send()
            first_gather(k).wait_send()
            last_gather(k).wait_send()
            last_project(k).wait_send()
        give(2).wait_send()
        give(3).wait_send()


def unpack(packed, beliefs_out, logs_out):
    frames = beliefs_out.shape[0]
    beliefs_out[...] = packed[:frames]
    logs_out[...] = packed[frames, :frames]


def solution(mesh):
    tiles = mesh.shape["tm"]
    assert mesh.shape["state"] == LAST + 1

    def per_device(symbols, emission, decay, left_factor, right_factor, initial):
        frames = symbols.shape[0]
        rank, cells = left_factor.shape[1:]
        pair_count = frames * (frames - 1) // 2
        sum_count = frames * (frames + 1) // 2
        base = pair_count * rank
        width = -(-(pair_count * rank + sum_count) // 128) * 128
        share = rank // tiles
        vmem, dma = pltpu.VMEM, pltpu.SemaphoreType.DMA
        others = tiles - 1
        packed = pl.pallas_call(
            functools.partial(kernel, tiles),
            out_shape=vmem((ROWS, cells), F32),
            in_specs=[pl.BlockSpec(memory_space=pltpu.SMEM)]
            + [pl.BlockSpec(memory_space=pltpu.HBM)] * 5,
            out_specs=pl.BlockSpec(memory_space=vmem),
            scratch_shapes=[
                vmem(emission.shape, F32),
                vmem(decay.shape, F32),
                vmem((rank, cells), F32),
                vmem((rank, cells), F32),
                vmem((1, cells), F32),
                vmem((width, cells), F32),
                vmem((tiles, share, base), F32),
                vmem((tiles, share, base), F32),
                vmem((share, base), F32),
                vmem((tiles, share, base), F32),
                vmem((rank, base), F32),
                vmem((tiles, share, width), F32),
                vmem((others, share, width), F32),
                vmem((share, width), F32),
                vmem((tiles, share, width), F32),
                vmem((rank, width), F32),
                vmem((ROWS, 128), F32),
                vmem((tiles, ROWS, 128), F32),
                vmem((others, ROWS, 128), F32),
                vmem((2 * frames, cells), F32),
                vmem((2 * frames, cells), F32),
                vmem((rank, cells), F32),
                vmem((ROWS, cells), F32),
                vmem((ROWS, cells), F32),
                vmem((ROWS, 128), F32),
                vmem((ROWS, 128), F32),
                dma((5,)),
                dma((tiles,)),
                dma((tiles,)),
                dma((others,)),
                dma((others,)),
                dma((others,)),
                dma((others,)),
                dma((others,)),
                dma((others,)),
                dma((tiles,)),
                dma((tiles,)),
                dma((others,)),
                dma((others,)),
                dma((4,)),
                dma((4,)),
                pltpu.SemaphoreType.REGULAR,
            ],
            compiler_params=pltpu.CompilerParams(collective_id=0, has_side_effects=True),
        )(symbols, emission, decay, left_factor, right_factor, initial.reshape(1, cells))
        return pl.pallas_call(
            unpack,
            out_shape=(
                jax.ShapeDtypeStruct((frames, cells), F32),
                jax.ShapeDtypeStruct((frames,), F32),
            ),
            in_specs=[pl.BlockSpec(memory_space=vmem)],
            out_specs=(pl.BlockSpec(memory_space=vmem),) * 2,
            compiler_params=pltpu.CompilerParams(vmem_limit_bytes=16 * 2**20),
        )(packed)

    return jax.shard_map(
        per_device,
        mesh=mesh,
        in_specs=(
            P("state"),
            P("tm", None),
            P("state", "tm"),
            P("state", None, "tm"),
            P("state", None, "tm"),
            P("tm"),
        ),
        out_specs=(P("state", "tm"), P("state")),
        check_vma=False,
    )
```

time: 26.7 us -> 24.3 us (0.910)
  the two profiles are of different devices: /device:TPU:1 before, /device:TPU:0 now
where the time goes in v3:
time: 24.3 us; the launch traced here: 24.1 us
  Pallas kernels  23.5 us (97%)
  between operations  0.64 us (3%)
    pallas_call x1, Pallas kernels, per_device(): pl.pallas_call(functools.partial(kernel, tiles), out_shape=vmem((ROWS, ce...  22.9 us
    pallas_call x1, Pallas kernels, per_device(): pl.pallas_call(unpack, out_shape=(jax.ShapeDtypeStruct((frames, cells), F...  0.6 us

profile of v3, /device:TPU:0, one launch (start us, length us, event | category | flops | bytes accessed | tf_op | source)
XLA Modules:
  0.0 24.1 jit_solution(13114335412176722193)
XLA Ops:
  0.6 22.9 %shard_map.77.packed = f32[8,512]{1,0:T(8,128)S(1)} custom-call(s32[4]{0:T(128)} %symbols.1, f32[512,256]{1,0:T(8,128)} %emission_hbm.1, f32[1,512]{1,0:T(1,128)} %decay_hbm.1, f32[1,64,512]{2,1,0:T(8,128)} %left_hbm.1, f32[1,64,512]{2,1,0:T(8,128)} %right_hbm.1, f32[1,512]{1,0:T(1,128)} %bitcast.1), custom_call_target="tpu_custom_call" | custom-call | tf_op jit(solution)/shard_map/pallas_call | solution.py:394
  23.5 0.6 %shard_map.78 = (f32[4,512]{1,0:T(4,128)}, f32[4]{0:T(128)}) custom-call(f32[8,512]{1,0:T(8,128)S(1)} %shard_map.77.packed), custom_call_target="tpu_custom_call" | custom-call | tf_op jit(solution)/shard_map/pallas_call | solution.py:446

commit v4 on v3

--- a/solution.py
+++ b/solution.py
@@ -61,12 +61,18 @@
     last_own,
     last_all,
     last_full,
+    first_row,
+    first_proj,
+    mid_rows,
+    mid_proj,
     pbuf,
-    first_proj,
     last_proj,
     pace,
     first_pace,
     first_right,
+    first_left,
+    lift_pieces,
+    probe_pieces,
     hand,
     handed,
     mass_out,
@@ -82,6 +88,8 @@
     lg_recv,
     fp_send,
     fp_recv,
+    mp_send,
+    mp_recv,
     lp_send,
     lp_recv,
     chip_send,
@@ -98,22 +106,10 @@
     sums = [(t, s) for s in range(frames) for t in range(s + 1, frames + 1)]
     base = len(pairs) * rank
     width = last_full.shape[1]
+    first_width = first_full.shape[1]
+    skip = (frames - 1) * rank // 128 * 128
     peers = [lax.rem(me + k, tiles) for k in range(tiles)]
     half = rank + 32
-
-    barrier = pltpu.get_barrier_semaphore()
-
-    @pl.when(span < LAST)
-    def _():
-        for k in range(tiles):
-            pl.semaphore_signal(barrier, inc=1, device_id={"tm": peers[k], "state": LAST})
-
-    @pl.when(span == LAST)
-    def _():
-        for k in range(1, tiles):
-            pl.semaphore_signal(barrier, inc=1, device_id={"tm": peers[k], "state": LAST})
-        for k in range(tiles):
-            pl.semaphore_signal(barrier, inc=1, device_id={"tm": peers[k], "state": 0})
 
     loads = [
         pltpu.make_async_copy(src, dst, load_sem.at[i])
@@ -130,6 +126,20 @@
     for load in loads:
         load.start()
 
+    barrier = pltpu.get_barrier_semaphore()
+
+    @pl.when(span < LAST)
+    def _():
+        for k in range(tiles):
+            pl.semaphore_signal(barrier, inc=1, device_id={"tm": peers[k], "state": LAST})
+
+    @pl.when(span == LAST)
+    def _():
+        for k in range(1, tiles):
+            pl.semaphore_signal(barrier, inc=1, device_id={"tm": peers[k], "state": LAST})
+        for k in range(tiles):
+            pl.semaphore_signal(barrier, inc=1, device_id={"tm": peers[k], "state": 0})
+
     def remote(src, dst, send, recv, tile, state):
         return pltpu.make_async_remote_copy(
             src, dst, send, recv, device_id={"tm": tile, "state": state}
@@ -137,36 +147,31 @@
 
     def first_scatter(k):
         return remote(
-            first_pieces.at[peers[k]], first_parts.at[k], fs_send.at[k], fs_recv.at[k], peers[k], LAST
+            first_pieces.at[peers[k]], first_parts.at[k], fs_send, fs_recv, peers[k], LAST
         )
 
     def first_project(k):
-        return remote(pbuf, first_proj.at[k], fp_send.at[k], fp_recv.at[k], peers[k], LAST)
+        return remote(first_row, first_proj.at[k], fp_send, fp_recv, peers[k], LAST)
 
     def first_gather(k):
-        return remote(
-            first_own, first_all.at[me], fg_send.at[k - 1], fg_recv.at[k - 1], peers[k], LAST
-        )
+        return remote(first_own, first_all.at[me], fg_send, fg_recv, peers[k], LAST)
+
+    def mid_project(k):
+        return remote(mid_rows, mid_proj.at[k - 1], mp_send, mp_recv, peers[k], LAST)
 
     def last_scatter(k):
         return remote(
-            last_pieces.at[peers[k]],
-            last_parts.at[k - 1],
-            ls_send.at[k - 1],
-            ls_recv.at[k - 1],
-            peers[k],
-            LAST,
+            last_pieces.at[peers[k]], last_parts.at[k - 1], ls_send, ls_recv, peers[k], LAST
         )
 
     def last_gather(k):
-        return remote(
-            last_own, last_all.at[me], lg_send.at[k - 1], lg_recv.at[k - 1], peers[k], LAST
-        )
+        return remote(last_own, last_all.at[me], lg_send, lg_recv, peers[k], LAST)
 
     def last_project(k):
-        return remote(
-            pbuf, last_proj.at[k - 1], lp_send.at[k - 1], lp_recv.at[k - 1], peers[k], LAST
-        )
+        return remote(pbuf, last_proj.at[k - 1], lp_send, lp_recv, peers[k], LAST)
+
+    def landed(ref, sem):
+        pltpu.make_async_copy(ref, ref, sem).wait()
 
     def give(i):
         src, dst, state = (
@@ -174,8 +179,11 @@
             (pace, first_pace, LAST),
             (hand, handed, 0),
             (mass_out, mass_in, 0),
+            (left, first_left, LAST),
         )[i]
         return remote(src, dst, chip_send.at[i], chip_recv.at[i], me, state)
+
+    others = pl.ds(0, tiles - 1)
 
     row_id = lax.broadcasted_iota(jnp.int32, (ROWS, emission.shape[1]), 0)
     column_id = lax.broadcasted_iota(jnp.int32, (ROWS, emission.shape[1]), 1)
@@ -197,13 +205,15 @@
         pace[t : t + 1] = emit[t]
         pace[frames + t : frames + t + 1] = grow[t]
 
+    def filled(rows):
+        return jnp.concatenate(rows + [jnp.zeros_like(rows[0])] * (ROWS - len(rows)), axis=0)
+
     def projections(row):
         rows = [row]
         for t in range(frames):
             row = row * grow[t]
             rows.append(row)
-        rows += [jnp.zeros_like(row)] * (ROWS - len(rows))
-        reached = jnp.concatenate(rows, axis=0)
+        reached = filled(rows)
         pbuf[:, :rank] = dot2(reached, scaled_pieces, ALONG)
         pbuf[:, rank:half] = jnp.broadcast_to(
             jnp.sum(reached, axis=1, keepdims=True), (ROWS, half - rank)
@@ -224,13 +234,13 @@
             side[base + i : base + i + 1] = reach[pair]
         return dot2(right[...], split(side[...]), ALONG)
 
-    def solve(mix, full):
+    def solve(mix, full, origin=0, start=0):
         mix_row = lax.broadcasted_iota(jnp.int32, mix.shape, 0)
         mix = jnp.where(mix_row < frames, mix, 0.0)
-        for s in range(frames - 1):
+        for s in range(start, frames - 1):
             for i, (t, u) in enumerate(pairs):
                 if u == s:
-                    matrix = split(full[:, i * rank : (i + 1) * rank])
+                    matrix = split(full[:, i * rank - origin : (i + 1) * rank - origin])
                     term = dot2(mix, matrix, ACROSS)[s : s + 1]
                     mix = mix + jnp.where(mix_row == t, term, 0.0)
         return mix
@@ -255,23 +265,24 @@
     @pl.when(span < LAST)
     def _():
         for j in range(tiles):
-            first_pieces[j] = coupling[j * share : (j + 1) * share, :base]
-        projections(entry[...])
-        pbuf[:, half:] = jnp.zeros((ROWS, pbuf.shape[1] - half), F32)
+            first_pieces[j] = coupling[j * share : (j + 1) * share, skip : skip + first_width]
+        row = entry[...]
+        first_row[:, :rank] = dot2(filled([row]), scaled_pieces, ALONG)[:1]
+        first_row[:, rank:] = jnp.broadcast_to(
+            jnp.sum(row, axis=1, keepdims=True), (1, first_row.shape[1] - rank)
+        )
         pl.semaphore_wait(barrier, tiles)
-        for k in range(tiles):
+        for k in reversed(range(tiles)):
+            first_project(k).start()
+        for k in reversed(range(tiles)):
             first_scatter(k).start()
-        for k in range(tiles):
-            first_project(k).start()
-        give(0).start()
-        give(1).start()
-        for k in range(tiles):
-            first_scatter(k).wait_send()
+        for i in (0, 1, 4):
+            give(i).start()
+        landed(first_pieces, fs_send)
         pl.semaphore_signal(clear, inc=1, device_id={"tm": me, "state": LAST})
-        for k in range(tiles):
-            first_project(k).wait_send()
-        give(0).wait_send()
-        give(1).wait_send()
+        landed(first_proj, fp_send)
+        for i in (0, 1, 4):
+            give(i).wait_send()
         give(2).wait_recv()
         kept = [handed[t : t + 1] for t in range(frames)]
         mass = [handed[frames : frames + 1, :1]]
@@ -288,38 +299,64 @@
         pl.semaphore_wait(clear, 1)
         for k in range(1, tiles):
             last_scatter(k).start()
-        total = jnp.zeros(first_own.shape, F32)
-        for k in range(tiles):
-            first_scatter(k).wait_recv()
+        for i in (0, 1, 4):
+            give(i).wait_recv()
+        for i, piece in enumerate(split(first_right[...])):
+            lift_pieces[i] = piece
+        for i, piece in enumerate(split(first_left[...] * (1.0 / states))):
+            probe_pieces[i] = piece
+        emits = [first_pace[t : t + 1] for t in range(frames)]
+        grows = [first_pace[frames + t : frames + t + 1] for t in range(frames)]
+        landed(first_proj, fp_recv)
+        opening = first_proj[0]
+        for k in range(1, tiles):
+            opening = opening + first_proj[k]
+        mix_first = jnp.broadcast_to(opening[:, :rank], (ROWS, rank))
+        lifted = dot2(mix_first, (lift_pieces[0], lift_pieces[1]), ACROSS)
+        second = grows[0] * entry[...] + emits[0] * lifted[:1]
+        rows = [second]
+        for t in range(1, frames - 1):
+            rows.append(rows[-1] * grows[t])
+        mid_rows[:, :rank] = dot2(filled(rows), (probe_pieces[0], probe_pieces[1]), ALONG)[
+            :frames
+        ]
+        mid_rows[:, rank:] = jnp.zeros((frames, mid_rows.shape[1] - rank), F32)
+        for k in range(1, tiles):
+            mid_project(k).start()
+        landed(first_parts, fs_recv)
+        total = first_parts[0]
+        for k in range(1, tiles):
             total = total + first_parts[k]
         first_own[...] = total
         for k in range(1, tiles):
             first_gather(k).start()
         first_all[me] = total
+        landed(last_parts, ls_recv)
         total = last_pieces[me]
         for k in range(1, tiles):
-            last_scatter(k).wait_recv()
             total = total + last_parts[k - 1]
         last_own[...] = total
         for k in range(1, tiles):
             last_gather(k).start()
         last_all[me] = total
 
-        projected = jnp.zeros(pbuf.shape, F32)
-        for k in range(tiles):
-            first_project(k).wait_recv()
-            projected = projected + first_proj[k]
-        give(0).wait_recv()
-        give(1).wait_recv()
-        for k in range(1, tiles):
-            first_gather(k).wait_recv()
+        landed(mid_proj, mp_recv)
+        later = mid_rows[...]
+        for k in range(1, tiles):
+            later = later + mid_proj[k - 1]
+        mix = jnp.concatenate(
+            [opening[:, :rank], later[: frames - 1, :rank]]
+            + [jnp.zeros((1, rank), F32)] * (ROWS - frames),
+            axis=0,
+        )
+        landed(first_all.at[others], fg_recv)
         for j in range(tiles):
             first_full[j * share : (j + 1) * share] = first_all[j]
-        mix = solve(projected[:, :rank], first_full)
-        lifted = dot2(mix, split(first_right[...]), ACROSS)
-        emits = [first_pace[t : t + 1] for t in range(frames)]
-        grows = [first_pace[frames + t : frames + t + 1] for t in range(frames)]
-        kept = advance(entry[...], emits, grows, lifted)
+        mix = solve(mix, first_full, skip, 1)
+        lifted = dot2(mix, (lift_pieces[0], lift_pieces[1]), ACROSS)
+        kept = [second]
+        for t in range(1, frames):
+            kept.append(grows[t] * kept[-1] + emits[t] * lifted[t : t + 1])
         belief = kept[-1]
         projections(belief)
         partial = jnp.concatenate(
@@ -332,16 +369,15 @@
             last_project(k).start()
         for t in range(frames):
             hand[t : t + 1] = kept[t]
-        hand[frames : frames + 1] = jnp.broadcast_to(projected[0:1, rank : rank + 1], (1, cells))
+        hand[frames : frames + 1] = jnp.broadcast_to(opening[:, rank : rank + 1], (1, cells))
         give(2).start()
 
-        for k in range(1, tiles):
-            last_gather(k).wait_recv()
+        landed(last_all.at[others], lg_recv)
         for j in range(tiles):
             last_full[j * share : (j + 1) * share] = last_all[j]
         projected = pbuf[...]
-        for k in range(1, tiles):
-            last_project(k).wait_recv()
+        landed(last_proj, lp_recv)
+        for k in range(1, tiles):
             projected = projected + last_proj[k - 1]
         mass_out[...] = projected
         give(3).start()
@@ -362,11 +398,11 @@
                 + jnp.sum(jnp.where(hit, parts, 0.0), keepdims=True)
             )
         write(kept, mass)
-        for k in range(1, tiles):
-            last_scatter(k).wait_send()
-            first_gather(k).wait_send()
-            last_gather(k).wait_send()
-            last_project(k).wait_send()
+        landed(last_parts, ls_send)
+        landed(first_all.at[others], fg_send)
+        landed(mid_proj, mp_send)
+        landed(last_all.at[others], lg_send)
+        landed(last_proj, lp_send)
         give(2).wait_send()
         give(3).wait_send()
 
@@ -387,6 +423,7 @@
         pair_count = frames * (frames - 1) // 2
         sum_count = frames * (frames + 1) // 2
         base = pair_count * rank
+        first_width = -(-base // 128) * 128 - (frames - 1) * rank // 128 * 128
         width = -(-(pair_count * rank + sum_count) // 128) * 128
         share = rank // tiles
         vmem, dma = pltpu.VMEM, pltpu.SemaphoreType.DMA
@@ -404,41 +441,36 @@
                 vmem((rank, cells), F32),
                 vmem((1, cells), F32),
                 vmem((width, cells), F32),
-                vmem((tiles, share, base), F32),
-                vmem((tiles, share, base), F32),
-                vmem((share, base), F32),
-                vmem((tiles, share, base), F32),
-                vmem((rank, base), F32),
+                vmem((tiles, share, first_width), F32),
+                vmem((tiles, share, first_width), F32),
+                vmem((share, first_width), F32),
+                vmem((tiles, share, first_width), F32),
+                vmem((rank, first_width), F32),
                 vmem((tiles, share, width), F32),
                 vmem((others, share, width), F32),
                 vmem((share, width), F32),
                 vmem((tiles, share, width), F32),
                 vmem((rank, width), F32),
+                vmem((1, 128), F32),
+                vmem((tiles, 1, 128), F32),
+                vmem((frames, 128), F32),
+                vmem((others, frames, 128), F32),
                 vmem((ROWS, 128), F32),
-                vmem((tiles, ROWS, 128), F32),
                 vmem((others, ROWS, 128), F32),
                 vmem((2 * frames, cells), F32),
                 vmem((2 * frames, cells), F32),
                 vmem((rank, cells), F32),
+                vmem((rank, cells), F32),
+                vmem((2, rank, cells), BF16),
+                vmem((2, rank, cells), BF16),
                 vmem((ROWS, cells), F32),
                 vmem((ROWS, cells), F32),
                 vmem((ROWS, 128), F32),
                 vmem((ROWS, 128), F32),
                 dma((5,)),
-                dma((tiles,)),
-                dma((tiles,)),
-                dma((others,)),
-                dma((others,)),
-                dma((others,)),
-                dma((others,)),
-                dma((others,)),
-                dma((others,)),
-                dma((tiles,)),
-                dma((tiles,)),
-                dma((others,)),
-                dma((others,)),
-                dma((4,)),
-                dma((4,)),
+                *[dma(())] * 14,
+                dma((5,)),
+                dma((5,)),
                 pltpu.SemaphoreType.REGULAR,
             ],
             compiler_params=pltpu.CompilerParams(collective_id=0, has_side_effects=True),

time: 24.3 us -> 22.5 us (0.926)
  Pallas kernels: 23.5 us -> 21.7 us
    pallas_call x1, Pallas kernels: 22.9 us -> 21.1 us  [per_device(): pl.pallas_call(functools.partial(kernel, tiles), out_shape=vmem((ROWS, ce...]
where the time goes in v4:
time: 22.5 us; the launch traced here: 22.4 us
  Pallas kernels  21.7 us (96%)
  between operations  0.64 us (3%)
    pallas_call x1, Pallas kernels, per_device(): pl.pallas_call(functools.partial(kernel, tiles), out_shape=vmem((ROWS, ce...  21.1 us
    pallas_call x1, Pallas kernels, per_device(): pl.pallas_call(unpack, out_shape=(jax.ShapeDtypeStruct((frames, cells), F...  0.6 us

profile of v4, /device:TPU:0, one launch (start us, length us, event | category | flops | bytes accessed | tf_op | source)
XLA Modules:
  0.0 22.4 jit_solution(18195099949822876873)
XLA Ops:
  0.6 21.1 %shard_map.77.packed = f32[8,512]{1,0:T(8,128)S(1)} custom-call(s32[4]{0:T(128)} %symbols.1, f32[512,256]{1,0:T(8,128)} %emission_hbm.1, f32[1,512]{1,0:T(1,128)} %decay_hbm.1, f32[1,64,512]{2,1,0:T(8,128)} %left_hbm.1, f32[1,64,512]{2,1,0:T(8,128)} %right_hbm.1, f32[1,512]{1,0:T(1,128)} %bitcast.1), custom_call_target="tpu_custom_call" | custom-call | tf_op jit(solution)/shard_map/pallas_call | solution.py:431
  21.8 0.6 %shard_map.78 = (f32[4,512]{1,0:T(4,128)}, f32[4]{0:T(128)}) custom-call(f32[8,512]{1,0:T(8,128)S(1)} %shard_map.77.packed), custom_call_target="tpu_custom_call" | custom-call | tf_op jit(solution)/shard_map/pallas_call | solution.py:478

commit v5 on v4

--- a/solution.py
+++ b/solution.py
@@ -73,6 +73,8 @@
     first_left,
     lift_pieces,
     probe_pieces,
+    solver,
+    sum_pieces,
     hand,
     handed,
     mass_out,
@@ -307,6 +309,14 @@
             probe_pieces[i] = piece
         emits = [first_pace[t : t + 1] for t in range(frames)]
         grows = [first_pace[frames + t : frames + t + 1] for t in range(frames)]
+        landed(first_parts, fs_recv)
+        total = first_parts[0]
+        for k in range(1, tiles):
+            total = total + first_parts[k]
+        first_own[...] = total
+        for k in range(1, tiles):
+            first_gather(k).start()
+        first_all[me] = total
         landed(first_proj, fp_recv)
         opening = first_proj[0]
         for k in range(1, tiles):
@@ -323,14 +333,6 @@
         mid_rows[:, rank:] = jnp.zeros((frames, mid_rows.shape[1] - rank), F32)
         for k in range(1, tiles):
             mid_project(k).start()
-        landed(first_parts, fs_recv)
-        total = first_parts[0]
-        for k in range(1, tiles):
-            total = total + first_parts[k]
-        first_own[...] = total
-        for k in range(1, tiles):
-            first_gather(k).start()
-        first_all[me] = total
         landed(last_parts, ls_recv)
         total = last_pieces[me]
         for k in range(1, tiles):
@@ -375,16 +377,42 @@
         landed(last_all.at[others], lg_recv)
         for j in range(tiles):
             last_full[j * share : (j + 1) * share] = last_all[j]
+        direct = {
+            pair: last_full[:, i * rank : (i + 1) * rank] for i, pair in enumerate(pairs)
+        }
+        direct_pieces = {pair: split(direct[pair]) for pair in pairs}
+        composed = {}
+        for reach in range(1, frames):
+            for t, u in pairs:
+                if t - u == reach:
+                    composed[t, u] = direct[t, u]
+                    for v in range(u + 1, t):
+                        composed[t, u] = composed[t, u] + dot2(
+                            composed[v, u], direct_pieces[t, v], ACROSS
+                        )
+        for i, pair in enumerate(pairs):
+            for j, piece in enumerate(split(composed[pair])):
+                solver[2 * i + j] = piece
+        for j, piece in enumerate(split(right[...])):
+            lift_pieces[j] = piece
+        for j, piece in enumerate(split(last_full[:, base:])):
+            sum_pieces[j] = piece
         projected = pbuf[...]
         landed(last_proj, lp_recv)
         for k in range(1, tiles):
             projected = projected + last_proj[k - 1]
         mass_out[...] = projected
         give(3).start()
-        mix = solve(projected[:, :rank], last_full)
-        lifted = dot2(mix, split(right[...]), ACROSS)
+        entering = projected[:, :rank]
+        mix_row = lax.broadcasted_iota(jnp.int32, entering.shape, 0)
+        entering = jnp.where(mix_row < frames, entering, 0.0)
+        mix = entering
+        for i, (t, u) in enumerate(pairs):
+            term = dot2(entering, (solver[2 * i], solver[2 * i + 1]), ACROSS)[u : u + 1]
+            mix = mix + jnp.where(mix_row == t, term, 0.0)
+        lifted = dot2(mix, (lift_pieces[0], lift_pieces[1]), ACROSS)
         kept = advance(belief, emit, grow, lifted)
-        parts = dot2(mix, split(last_full[:, base:]), ACROSS)
+        parts = dot2(mix, (sum_pieces[0], sum_pieces[1]), ACROSS)
         part_row = lax.broadcasted_iota(jnp.int32, parts.shape, 0)
         part_column = lax.broadcasted_iota(jnp.int32, parts.shape, 1)
         mass = [projected[0:1, rank : rank + 1]]
@@ -463,6 +491,8 @@
                 vmem((rank, cells), F32),
                 vmem((2, rank, cells), BF16),
                 vmem((2, rank, cells), BF16),
+                vmem((2 * pair_count, rank, rank), BF16),
+                vmem((2, rank, width - base), BF16),
                 vmem((ROWS, cells), F32),
                 vmem((ROWS, cells), F32),
                 vmem((ROWS, 128), F32),

time: 22.5 us -> 22.9 us (1.018)
  Pallas kernels: 21.7 us -> 22.1 us
    pallas_call x1, Pallas kernels: 21.1 us -> 21.5 us  [per_device(): pl.pallas_call(functools.partial(kernel, tiles), out_shape=vmem((ROWS, ce...]
where the time goes in v5:
time: 22.9 us; the launch traced here: 22.7 us
  Pallas kernels  22.1 us (97%)
  between operations  0.64 us (3%)
    pallas_call x1, Pallas kernels, per_device(): pl.pallas_call(functools.partial(kernel, tiles), out_shape=vmem((ROWS, ce...  21.5 us
    pallas_call x1, Pallas kernels, per_device(): pl.pallas_call(unpack, out_shape=(jax.ShapeDtypeStruct((frames, cells), F...  0.6 us

profile of v5, /device:TPU:0, one launch (start us, length us, event | category | flops | bytes accessed | tf_op | source)
XLA Modules:
  0.0 22.7 jit_solution(9655142852493974992)
XLA Ops:
  0.6 21.5 %shard_map.77.packed = f32[8,512]{1,0:T(8,128)S(1)} custom-call(s32[4]{0:T(128)} %symbols.1, f32[512,256]{1,0:T(8,128)} %emission_hbm.1, f32[1,512]{1,0:T(1,128)} %decay_hbm.1, f32[1,64,512]{2,1,0:T(8,128)} %left_hbm.1, f32[1,64,512]{2,1,0:T(8,128)} %right_hbm.1, f32[1,512]{1,0:T(1,128)} %bitcast.1), custom_call_target="tpu_custom_call" | custom-call | tf_op jit(solution)/shard_map/pallas_call | solution.py:459
  22.1 0.6 %shard_map.78 = (f32[4,512]{1,0:T(4,128)}, f32[4]{0:T(128)}) custom-call(f32[8,512]{1,0:T(8,128)S(1)} %shard_map.77.packed), custom_call_target="tpu_custom_call" | custom-call | tf_op jit(solution)/shard_map/pallas_call | solution.py:508

commit v6 on v5

--- a/solution.py
+++ b/solution.py
@@ -309,14 +309,6 @@
             probe_pieces[i] = piece
         emits = [first_pace[t : t + 1] for t in range(frames)]
         grows = [first_pace[frames + t : frames + t + 1] for t in range(frames)]
-        landed(first_parts, fs_recv)
-        total = first_parts[0]
-        for k in range(1, tiles):
-            total = total + first_parts[k]
-        first_own[...] = total
-        for k in range(1, tiles):
-            first_gather(k).start()
-        first_all[me] = total
         landed(first_proj, fp_recv)
         opening = first_proj[0]
         for k in range(1, tiles):
@@ -333,6 +325,14 @@
         mid_rows[:, rank:] = jnp.zeros((frames, mid_rows.shape[1] - rank), F32)
         for k in range(1, tiles):
             mid_project(k).start()
+        landed(first_parts, fs_recv)
+        total = first_parts[0]
+        for k in range(1, tiles):
+            total = total + first_parts[k]
+        first_own[...] = total
+        for k in range(1, tiles):
+            first_gather(k).start()
+        first_all[me] = total
         landed(last_parts, ls_recv)
         total = last_pieces[me]
         for k in range(1, tiles):

time: 22.9 us -> 22.5 us (0.983)
  Pallas kernels: 22.1 us -> 21.7 us
    pallas_call x1, Pallas kernels: 21.5 us -> 21.1 us  [per_device(): pl.pallas_call(functools.partial(kernel, tiles), out_shape=vmem((ROWS, ce...]
where the time goes in v6:
time: 22.5 us; the launch traced here: 22.4 us
  Pallas kernels  21.7 us (96%)
  between operations  0.64 us (3%)
    pallas_call x1, Pallas kernels, per_device(): pl.pallas_call(functools.partial(kernel, tiles), out_shape=vmem((ROWS, ce...  21.1 us
    pallas_call x1, Pallas kernels, per_device(): pl.pallas_call(unpack, out_shape=(jax.ShapeDtypeStruct((frames, cells), F...  0.6 us

profile of v6, /device:TPU:0, one launch (start us, length us, event | category | flops | bytes accessed | tf_op | source)
XLA Modules:
  0.0 22.4 jit_solution(4988615974119861542)
XLA Ops:
  0.6 21.1 %shard_map.77.packed = f32[8,512]{1,0:T(8,128)S(1)} custom-call(s32[4]{0:T(128)} %symbols.1, f32[512,256]{1,0:T(8,128)} %emission_hbm.1, f32[1,512]{1,0:T(1,128)} %decay_hbm.1, f32[1,64,512]{2,1,0:T(8,128)} %left_hbm.1, f32[1,64,512]{2,1,0:T(8,128)} %right_hbm.1, f32[1,512]{1,0:T(1,128)} %bitcast.1), custom_call_target="tpu_custom_call" | custom-call | tf_op jit(solution)/shard_map/pallas_call | solution.py:459
  21.8 0.6 %shard_map.78 = (f32[4,512]{1,0:T(4,128)}, f32[4]{0:T(128)}) custom-call(f32[8,512]{1,0:T(8,128)S(1)} %shard_map.77.packed), custom_call_target="tpu_custom_call" | custom-call | tf_op jit(solution)/shard_map/pallas_call | solution.py:508
